TPU v7x, 8 devices: a whole 2x2x1 slice. The times are simulated.
8 devices in a mesh: part: 1 (over z), data: 2 (over y), time: 4 (over x, core).
Axes of the slice: x: 2, y: 2, z: 1, core: 2. Of those that a mesh axis runs over, the one named last changes fastest.
Arguments:
- x_init: float32 [4, 256, 16], P(('part', 'data'))
- w_in: bfloat16 [16, 1152], replicated
- w_out: bfloat16 [1152, 16], replicated
- mod_scale: bfloat16 [16, 1152], P('time')
- mod_shift: bfloat16 [16, 1152], P('time')
- step_size: float32 [16], P('time')
Outputs:
- output: float32 [16, 4, 256, 16], P('time', ('part', 'data'))
All inputs are finite; a program needn't handle non-finite values.
Results may differ from a plain program's by a relative error of at most 0.001.
Values are sent between devices in bfloat16 or wider.
A program may use at most 1 GiB of HBM per device.

v0:
```python
import jax
import jax.numpy as jnp
from jax import lax
from jax.sharding import PartitionSpec as P

SWEEPS = 4


def drift_of(latents, w_in, w_out, scale_one, shift_val, step_size):
    pre = jnp.einsum("kbnc,ch->kbnh", latents.astype(jnp.bfloat16), w_in, preferred_element_type=jnp.float32)
    act = jax.nn.gelu(pre * scale_one[:, None, None, :] + shift_val[:, None, None, :], approximate=True)
    out = jnp.einsum("kbnh,hc->kbnc", act.astype(jnp.bfloat16), w_out, preferred_element_type=jnp.float32)
    return out * step_size[:, None, None, None]


def solution(mesh):
    time_size = mesh.shape["time"]
    hop_shifts = [1 << level for level in range(32) if (1 << level) < time_size]

    def local_run(x_init, w_in, w_out, mod_scale, mod_shift, step_size):
        scale_one = 1.0 + mod_scale.astype(jnp.float32)
        shift_val = mod_shift.astype(jnp.float32)
        latents = jnp.broadcast_to(x_init[None], (step_size.shape[0],) + x_init.shape)
        for sweep_index in range(SWEEPS):
            drift = drift_of(latents, w_in, w_out, scale_one, shift_val, step_size)
            running = jnp.cumsum(drift, axis=0)
            dev_total = running[-1]
            inclusive = dev_total
            for hop_shift in hop_shifts:
                pairs = [(source, source + hop_shift) for source in range(time_size - hop_shift)]
                inclusive = inclusive + lax.ppermute(inclusive, "time", pairs)
            offset = inclusive - dev_total
            latents = x_init[None] + offset[None] + (running - drift)
        return latents

    return jax.shard_map(
        local_run,
        mesh=mesh,
        in_specs=(P(("part", "data"), None, None), P(None, None), P(None, None), P("time", None), P("time", None), P("time")),
        out_specs=P("time", ("part", "data"), None, None),
        check_vma=False,
    )
```

profile of v0, /device:TPU:0, one launch (start us, length us, event | category | flops | bytes accessed | tf_op | source)
XLA Modules:
  0.0 67.3 jit_solution(7263122578535590438)
XLA Ops:
  0.0 0.0 copy-start
  0.0 0.8 %convert_element_type.31 = bf16[2,256,16]{1,2,0:T(8,128)(2,1)S(1)} convert(f32[2,256,16]{1,2,0:T(8,128)} %param.6) | non-fusion elementwise | flops 8192 | bytes 49152 | tf_op jit(solution)/shard_map/convert_element_type | solution.py:10
  0.8 0.7 %convert_add_fusion = f32[4,1152]{1,0:T(4,128)S(1)} fusion(bf16[4,1152]{1,0:T(4,128)(2,1)} %param.9), kind=kLoop, calls=%fused_computation.68 | loop fusion | flops 9216 | bytes 27648 | tf_op jit(solution)/shard_map/add | solution.py:21
  1.5 0.7 %convert_element_type.33 = f32[4,1152]{1,0:T(4,128)S(1)} convert(bf16[4,1152]{1,0:T(4,128)(2,1)} %param.10) | non-fusion elementwise | flops 4608 | bytes 27648 | tf_op jit(solution)/shard_map/convert_element_type | solution.py:22
  2.2 0.0 copy-done
  2.2 4.8 %fusion.36 = f32[4,2,256,16]{2,3,1,0:T(8,128)S(1)} fusion(f32[4,1152]{1,0:T(4,128)S(1)} %convert_element_type.33, f32[4,1152]{1,0:T(4,128)S(1)} %convert_add_fusion, f32[4]{0:T(128)} %param.11, bf16[1152,16]{0,1:T(8,128)(2,1)S(1)} %copy-done, bf16[16,1152]{1,0:T(8,128)(2,1)} %param.7, bf16[2,256,16]{1,2,0:T(8,128)(2,1)S(1)} %convert_element_type.31), kind=kOutput, calls=%fused_computation.40 | convolution fusion | flops 176979968 | bytes 258064 | tf_op jit(solution)/shard_map/kbnh,hc->kbnc/dot_general | solution.py:12
  7.0 0.5 fusion.80
  7.5 0.0 copy-start.1
  7.6 0.0 copy-start.2
  7.6 0.0 copy-start.3
  7.6 2.8 %collective-permute-start = (f32[2,256,16]{1,2,0:T(8,128)S(1)}, f32[2,256,16]{1,2,0:T(8,128)S(1)}, u32[]{:S(2)}, u32[]{:S(2)}) collective-permute-start(f32[2,256,16]{1,2,0:T(8,128)S(1)} %slice_bitcast_fusion.3), channel_id=1, source_target_pairs={{0,1},{1,2},{2,3},{4,5},{5,6},{6,7}} | collective-permute-start | bytes 98312 | tf_op jit(solution)/shard_map/ppermute | solution.py:31
  10.4 0.8 %collective-permute-done = f32[2,256,16]{1,2,0:T(8,128)S(1)} collective-permute-done((f32[2,256,16]{1,2,0:T(8,128)S(1)}, f32[2,256,16]{1,2,0:T(8,128)S(1)}, u32[]{:S(2)}, u32[]{:S(2)}) %collective-permute-start) | collective-permute-done | bytes 32800 | tf_op jit(solution)/shard_map/ppermute | solution.py:31
  11.2 6.8 %collective-permute-start.1 = (f32[2,256,16]{1,2,0:T(8,128)S(1)}, f32[2,256,16]{1,2,0:T(8,128)S(1)}, u32[]{:S(2)}, u32[]{:S(2)}) collective-permute-start(f32[2,256,16]{1,2,0:T(8,128)S(1)} %fusion.76), channel_id=1, source_target_pairs={{0,2},{1,3},{4,6},{5,7}} | collective-permute-start | bytes 98312 | tf_op jit(solution)/shard_map/ppermute | solution.py:31
  18.1 1.6 %collective-permute-done.1 = f32[2,256,16]{1,2,0:T(8,128)S(1)} collective-permute-done((f32[2,256,16]{1,2,0:T(8,128)S(1)}, f32[2,256,16]{1,2,0:T(8,128)S(1)}, u32[]{:S(2)}, u32[]{:S(2)}) %collective-permute-start.1) | collective-permute-done | bytes 32800 | tf_op jit(solution)/shard_map/ppermute | solution.py:31
  19.6 0.0 copy-done.1
  19.7 0.0 copy-done.2
  19.7 0.0 copy-done.3
  19.7 4.1 %fusion.37 = f32[4,2,256,16]{2,3,1,0:T(8,128)S(1)} fusion(f32[4,1152]{1,0:T(4,128)S(1)} %convert_element_type.33, f32[4,1152]{1,0:T(4,128)S(1)} %convert_add_fusion, f32[4,2,256,16]{2,3,1,0:T(8,128)S(1)} %fusion.80, f32[4,2,256,16]{2,3,1,0:T(8,128)S(1)} %fusion.36, f32[2,256,16]{1,2,0:T(8,128)S(1)} %subtract_add_fusion.4, f32[4]{0:T(128)S(1)} %copy-done.3, ...), kind=kOutput, calls=%fused_computation.41 | convolution fusion | flops 177078272 | bytes 536592 | tf_op jit(solution)/shard_map/kbnh,hc->kbnc/dot_general | solution.py:12
  23.7 0.5 fusion.81
  24.3 1.3 %collective-permute-start.2 = (f32[2,256,16]{1,2,0:T(8,128)S(1)}, f32[2,256,16]{1,2,0:T(8,128)S(1)}, u32[]{:S(2)}, u32[]{:S(2)}) collective-permute-start(f32[2,256,16]{1,2,0:T(8,128)S(1)} %slice_bitcast_fusion.2), channel_id=1, source_target_pairs={{0,1},{1,2},{2,3},{4,5},{5,6},{6,7}} | collective-permute-start | bytes 98312 | tf_op jit(solution)/shard_map/ppermute | solution.py:31
  25.6 0.8 %collective-permute-done.2 = f32[2,256,16]{1,2,0:T(8,128)S(1)} collective-permute-done((f32[2,256,16]{1,2,0:T(8,128)S(1)}, f32[2,256,16]{1,2,0:T(8,128)S(1)}, u32[]{:S(2)}, u32[]{:S(2)}) %collective-permute-start.2) | collective-permute-done | bytes 32800 | tf_op jit(solution)/shard_map/ppermute | solution.py:31
  26.4 7.5 %collective-permute-start.3 = (f32[2,256,16]{1,2,0:T(8,128)S(1)}, f32[2,256,16]{1,2,0:T(8,128)S(1)}, u32[]{:S(2)}, u32[]{:S(2)}) collective-permute-start(f32[2,256,16]{1,2,0:T(8,128)S(1)} %fusion.77), channel_id=1, source_target_pairs={{0,2},{1,3},{4,6},{5,7}} | collective-permute-start | bytes 98312 | tf_op jit(solution)/shard_map/ppermute | solution.py:31
  33.9 1.4 %collective-permute-done.3 = f32[2,256,16]{1,2,0:T(8,128)S(1)} collective-permute-done((f32[2,256,16]{1,2,0:T(8,128)S(1)}, f32[2,256,16]{1,2,0:T(8,128)S(1)}, u32[]{:S(2)}, u32[]{:S(2)}) %collective-permute-start.3) | collective-permute-done | bytes 32800 | tf_op jit(solution)/shard_map/ppermute | solution.py:31
  35.3 4.1 %fusion.38 = f32[4,2,256,16]{2,3,1,0:T(8,128)S(1)} fusion(f32[4,1152]{1,0:T(4,128)S(1)} %convert_element_type.33, f32[4,1152]{1,0:T(4,128)S(1)} %convert_add_fusion, f32[4,2,256,16]{2,3,1,0:T(8,128)S(1)} %fusion.81, f32[4,2,256,16]{2,3,1,0:T(8,128)S(1)} %fusion.37, f32[2,256,16]{1,2,0:T(8,128)S(1)} %subtract_add_fusion.3, f32[4]{0:T(128)S(1)} %copy-done.3, ...), kind=kOutput, calls=%fused_computation.42 | convolution fusion | flops 177078272 | bytes 536592 | tf_op jit(solution)/shard_map/kbnh,hc->kbnc/dot_general | solution.py:12
  39.4 0.5 fusion.82
  39.9 1.3 %collective-permute-start.4 = (f32[2,256,16]{1,2,0:T(8,128)S(1)}, f32[2,256,16]{1,2,0:T(8,128)S(1)}, u32[]{:S(2)}, u32[]{:S(2)}) collective-permute-start(f32[2,256,16]{1,2,0:T(8,128)S(1)} %slice_bitcast_fusion.1), channel_id=1, source_target_pairs={{0,1},{1,2},{2,3},{4,5},{5,6},{6,7}} | collective-permute-start | bytes 98312 | tf_op jit(solution)/shard_map/ppermute | solution.py:31
  41.2 0.8 %collective-permute-done.4 = f32[2,256,16]{1,2,0:T(8,128)S(1)} collective-permute-done((f32[2,256,16]{1,2,0:T(8,128)S(1)}, f32[2,256,16]{1,2,0:T(8,128)S(1)}, u32[]{:S(2)}, u32[]{:S(2)}) %collective-permute-start.4) | collective-permute-done | bytes 32800 | tf_op jit(solution)/shard_map/ppermute | solution.py:31
  42.0 7.3 %collective-permute-start.5 = (f32[2,256,16]{1,2,0:T(8,128)S(1)}, f32[2,256,16]{1,2,0:T(8,128)S(1)}, u32[]{:S(2)}, u32[]{:S(2)}) collective-permute-start(f32[2,256,16]{1,2,0:T(8,128)S(1)} %fusion.78), channel_id=1, source_target_pairs={{0,2},{1,3},{4,6},{5,7}} | collective-permute-start | bytes 98312 | tf_op jit(solution)/shard_map/ppermute | solution.py:31
  49.4 1.6 %collective-permute-done.5 = f32[2,256,16]{1,2,0:T(8,128)S(1)} collective-permute-done((f32[2,256,16]{1,2,0:T(8,128)S(1)}, f32[2,256,16]{1,2,0:T(8,128)S(1)}, u32[]{:S(2)}, u32[]{:S(2)}) %collective-permute-start.5) | collective-permute-done | bytes 32800 | tf_op jit(solution)/shard_map/ppermute | solution.py:31
  51.0 4.1 %fusion.39 = f32[4,2,256,16]{2,3,1,0:T(8,128)S(1)} fusion(f32[4,1152]{1,0:T(4,128)S(1)} %convert_element_type.33, f32[4,1152]{1,0:T(4,128)S(1)} %convert_add_fusion, f32[4,2,256,16]{2,3,1,0:T(8,128)S(1)} %fusion.82, f32[4,2,256,16]{2,3,1,0:T(8,128)S(1)} %fusion.38, f32[2,256,16]{1,2,0:T(8,128)S(1)} %subtract_add_fusion.2, f32[4]{0:T(128)S(1)} %copy-done.3, ...), kind=kOutput, calls=%fused_computation.43 | convolution fusion | flops 177078272 | bytes 536592 | tf_op jit(solution)/shard_map/kbnh,hc->kbnc/dot_general | solution.py:12
  55.0 0.5 fusion.83
  55.5 1.3 %collective-permute-start.6 = (f32[2,256,16]{1,2,0:T(8,128)S(1)}, f32[2,256,16]{1,2,0:T(8,128)S(1)}, u32[]{:S(2)}, u32[]{:S(2)}) collective-permute-start(f32[2,256,16]{1,2,0:T(8,128)S(1)} %slice_bitcast_fusion), channel_id=1, source_target_pairs={{0,1},{1,2},{2,3},{4,5},{5,6},{6,7}} | collective-permute-start | bytes 98312 | tf_op jit(solution)/shard_map/ppermute | solution.py:31
  56.8 0.8 %collective-permute-done.6 = f32[2,256,16]{1,2,0:T(8,128)S(1)} collective-permute-done((f32[2,256,16]{1,2,0:T(8,128)S(1)}, f32[2,256,16]{1,2,0:T(8,128)S(1)}, u32[]{:S(2)}, u32[]{:S(2)}) %collective-permute-start.6) | collective-permute-done | bytes 32800 | tf_op jit(solution)/shard_map/ppermute | solution.py:31
  57.7 7.3 %collective-permute-start.7 = (f32[2,256,16]{1,2,0:T(8,128)S(1)}, f32[2,256,16]{1,2,0:T(8,128)S(1)}, u32[]{:S(2)}, u32[]{:S(2)}) collective-permute-start(f32[2,256,16]{1,2,0:T(8,128)S(1)} %fusion.79), channel_id=1, source_target_pairs={{0,2},{1,3},{4,6},{5,7}} | collective-permute-start | bytes 98312 | tf_op jit(solution)/shard_map/ppermute | solution.py:31
  65.0 1.6 %collective-permute-done.7 = f32[2,256,16]{1,2,0:T(8,128)S(1)} collective-permute-done((f32[2,256,16]{1,2,0:T(8,128)S(1)}, f32[2,256,16]{1,2,0:T(8,128)S(1)}, u32[]{:S(2)}, u32[]{:S(2)}) %collective-permute-start.7) | collective-permute-done | bytes 32800 | tf_op jit(solution)/shard_map/ppermute | solution.py:31
  66.6 0.7 %subtract_add_fusion = f32[4,2,256,16]{2,3,1,0:T(8,128)} fusion(f32[4,2,256,16]{2,3,1,0:T(8,128)S(1)} %fusion.83, f32[4,2,256,16]{2,3,1,0:T(8,128)S(1)} %fusion.39, f32[2,256,16]{1,2,0:T(8,128)S(1)} %subtract_add_fusion.1), kind=kLoop, calls=%fused_computation.44 | loop fusion | flops 65536 | bytes 425984 | tf_op jit(solution)/shard_map/add | solution.py:33
  (12 shorter events, 0.1 us)
Async XLA Ops:
  0.0 2.2 %copy-start = (bf16[1152,16]{0,1:T(8,128)(2,1)S(1)}, bf16[1152,16]{0,1:T(8,128)(2,1)}, u32[]{:S(2)}) copy-start(bf16[1152,16]{0,1:T(8,128)(2,1)} %param.8) | copy-start | bytes 110596
  7.5 12.1 %copy-start.1 = (f32[2,256,16]{1,2,0:T(8,128)S(1)}, f32[2,256,16]{1,2,0:T(8,128)}, u32[]{:S(2)}) copy-start(f32[2,256,16]{1,2,0:T(8,128)} %param.6) | copy-start | bytes 98308
  7.6 12.1 %copy-start.2 = (bf16[16,1152]{1,0:T(8,128)(2,1)S(1)}, bf16[16,1152]{1,0:T(8,128)(2,1)}, u32[]{:S(2)}) copy-start(bf16[16,1152]{1,0:T(8,128)(2,1)} %param.7) | copy-start | bytes 110596
  7.6 12.1 %copy-start.3 = (f32[4]{0:T(128)S(1)}, f32[4]{0:T(128)}, u32[]{:S(2)}) copy-start(f32[4]{0:T(128)} %param.11) | copy-start | bytes 52
  7.6 3.6 %collective-permute-start = (f32[2,256,16]{1,2,0:T(8,128)S(1)}, f32[2,256,16]{1,2,0:T(8,128)S(1)}, u32[]{:S(2)}, u32[]{:S(2)}) collective-permute-start(f32[2,256,16]{1,2,0:T(8,128)S(1)} %slice_bitcast_fusion.3), channel_id=1, source_target_pairs={{0,1},{1,2},{2,3},{4,5},{5,6},{6,7}} | collective-permute-start | bytes 98312 | tf_op jit(solution)/shard_map/ppermute | solution.py:31
  11.2 8.4 %collective-permute-start.1 = (f32[2,256,16]{1,2,0:T(8,128)S(1)}, f32[2,256,16]{1,2,0:T(8,128)S(1)}, u32[]{:S(2)}, u32[]{:S(2)}) collective-permute-start(f32[2,256,16]{1,2,0:T(8,128)S(1)} %fusion.76), channel_id=1, source_target_pairs={{0,2},{1,3},{4,6},{5,7}} | collective-permute-start | bytes 98312 | tf_op jit(solution)/shard_map/ppermute | solution.py:31
  24.3 2.1 %collective-permute-start.2 = (f32[2,256,16]{1,2,0:T(8,128)S(1)}, f32[2,256,16]{1,2,0:T(8,128)S(1)}, u32[]{:S(2)}, u32[]{:S(2)}) collective-permute-start(f32[2,256,16]{1,2,0:T(8,128)S(1)} %slice_bitcast_fusion.2), channel_id=1, source_target_pairs={{0,1},{1,2},{2,3},{4,5},{5,6},{6,7}} | collective-permute-start | bytes 98312 | tf_op jit(solution)/shard_map/ppermute | solution.py:31
  26.4 8.9 %collective-permute-start.3 = (f32[2,256,16]{1,2,0:T(8,128)S(1)}, f32[2,256,16]{1,2,0:T(8,128)S(1)}, u32[]{:S(2)}, u32[]{:S(2)}) collective-permute-start(f32[2,256,16]{1,2,0:T(8,128)S(1)} %fusion.77), channel_id=1, source_target_pairs={{0,2},{1,3},{4,6},{5,7}} | collective-permute-start | bytes 98312 | tf_op jit(solution)/shard_map/ppermute | solution.py:31
  39.9 2.1 %collective-permute-start.4 = (f32[2,256,16]{1,2,0:T(8,128)S(1)}, f32[2,256,16]{1,2,0:T(8,128)S(1)}, u32[]{:S(2)}, u32[]{:S(2)}) collective-permute-start(f32[2,256,16]{1,2,0:T(8,128)S(1)} %slice_bitcast_fusion.1), channel_id=1, source_target_pairs={{0,1},{1,2},{2,3},{4,5},{5,6},{6,7}} | collective-permute-start | bytes 98312 | tf_op jit(solution)/shard_map/ppermute | solution.py:31
  42.0 8.9 %collective-permute-start.5 = (f32[2,256,16]{1,2,0:T(8,128)S(1)}, f32[2,256,16]{1,2,0:T(8,128)S(1)}, u32[]{:S(2)}, u32[]{:S(2)}) collective-permute-start(f32[2,256,16]{1,2,0:T(8,128)S(1)} %fusion.78), channel_id=1, source_target_pairs={{0,2},{1,3},{4,6},{5,7}} | collective-permute-start | bytes 98312 | tf_op jit(solution)/shard_map/ppermute | solution.py:31
  55.5 2.1 %collective-permute-start.6 = (f32[2,256,16]{1,2,0:T(8,128)S(1)}, f32[2,256,16]{1,2,0:T(8,128)S(1)}, u32[]{:S(2)}, u32[]{:S(2)}) collective-permute-start(f32[2,256,16]{1,2,0:T(8,128)S(1)} %slice_bitcast_fusion), channel_id=1, source_target_pairs={{0,1},{1,2},{2,3},{4,5},{5,6},{6,7}} | collective-permute-start | bytes 98312 | tf_op jit(solution)/shard_map/ppermute | solution.py:31
  57.7 8.9 %collective-permute-start.7 = (f32[2,256,16]{1,2,0:T(8,128)S(1)}, f32[2,256,16]{1,2,0:T(8,128)S(1)}, u32[]{:S(2)}, u32[]{:S(2)}) collective-permute-start(f32[2,256,16]{1,2,0:T(8,128)S(1)} %fusion.79), channel_id=1, source_target_pairs={{0,2},{1,3},{4,6},{5,7}} | collective-permute-start | bytes 98312 | tf_op jit(solution)/shard_map/ppermute | solution.py:31
where the time goes:
time: 67.8 us; the launch traced here: 67.3 us
  starting transfers between devices  35.6 us (53%)
  matrix products  17 us (25%)
  waiting for transfers between devices  9.5 us (14%)
  other arithmetic  4.98 us (7%)
    ppermute x8, starting transfers between devices, local_run(): inclusive = inclusive + lax.ppermute(inclusive, 'time', pairs)  35.6 us
    dot_general x4, matrix products, drift_of(): jnp.einsum('kbnh,hc->kbnc', act.astype(jnp.bfloat16), w_out, preferred_el...  17 us
    ppermute x8, waiting for transfers between devices, local_run(): inclusive = inclusive + lax.ppermute(inclusive, 'time', pairs)  9.5 us
    another operation x4, other arithmetic, local_run(): running = jnp.cumsum(drift, axis=0)  2.06 us
  transfers between devices with their start and end apart: 8, of which 8 were waited for; matrix products, arithmetic and copies ran while one was open for 0% of the time, Pallas kernels for 0%

commit v1 on v0

v1 whole, which is shorter than its diff:
```python
import functools
import math

import jax
import jax.numpy as jnp
from jax import lax
from jax.experimental import pallas as pl
from jax.experimental.pallas import tpu as pltpu
from jax.sharding import PartitionSpec as P

SWEEPS = 4
LANES = 128
ROWS = 128
MESH = pl.DeviceIdType.MESH

A = 2.0 * math.sqrt(2.0 / math.pi)
B = 8.0 * math.sqrt(2.0 / math.pi) * 0.044715


def kernel(
    x_hbm, win_hbm, wout_hbm, scale_hbm, shift_hbm, step_hbm, out_ref,
    xv, win, wout, mods, steps, weights, drifts, stage,
    local_sem, mod_send, mod_recv, step_send, step_recv, out_send, out_recv,
):
    me = lax.axis_index("time")
    n_dev = 4
    per_dev = mods.shape[2]
    hidden = win.shape[1]
    partner = me + 1 - 2 * lax.rem(me, 2)
    order = [me, partner, lax.rem(me + 2, n_dev), lax.rem(partner + 2, n_dev)]
    peers = order[1:]

    barrier = pltpu.get_barrier_semaphore()
    for peer in peers:
        pl.semaphore_signal(barrier, inc=1, device_id={"time": peer}, device_id_type=MESH)

    sample = me // 2
    first = pl.multiple_of(lax.rem(me, 2) * LANES, LANES)
    loads = [
        pltpu.make_async_copy(scale_hbm, mods.at[me, 0], local_sem.at[0]),
        pltpu.make_async_copy(shift_hbm, mods.at[me, 1], local_sem.at[1]),
        pltpu.make_async_copy(step_hbm, steps.at[me], local_sem.at[2]),
        pltpu.make_async_copy(win_hbm, win, local_sem.at[3]),
        pltpu.make_async_copy(x_hbm.at[sample, :, pl.ds(first, LANES)], xv, local_sem.at[4]),
        pltpu.make_async_copy(wout_hbm, wout, local_sem.at[5]),
    ]
    for load in loads:
        load.start()
    for load in loads:
        load.wait()
    pl.semaphore_wait(barrier, len(peers))

    sends = []
    for peer in peers:
        for ref, send, recv in ((mods, mod_send, mod_recv), (steps, step_send, step_recv)):
            copy = pltpu.make_async_remote_copy(
                src_ref=ref.at[me], dst_ref=ref.at[me], send_sem=send.at[peer], recv_sem=recv.at[me],
                device_id={"time": peer}, device_id_type=MESH)
            copy.start()
            sends.append(copy)

    win_b = win[...]
    win_f = win_b.astype(jnp.float32)
    wout_b = wout[...]
    zero = jnp.zeros((16, LANES), jnp.bfloat16)
    row = lax.broadcasted_iota(jnp.int32, (16, LANES), 0)
    unit = jnp.where(row == 0, 0.5, 0.0).astype(jnp.bfloat16)

    def rhs_of(left, right):
        columns = []
        for at, value in enumerate((left, right)):
            if value is None:
                continue
            half = (value * 0.5).astype(jnp.bfloat16)
            own = [half, half, half, unit]
            blank = [zero] * 4
            columns.append(jnp.concatenate(own + blank if at == 0 else blank + own, axis=0))
        return columns[0] if len(columns) == 1 else jnp.concatenate(columns, axis=1)

    def drift_of(pair, rhs):
        total = None
        for at in range(0, hidden, ROWS):
            half = jnp.dot(weights[pair, at:at + ROWS, :], rhs, preferred_element_type=jnp.float32)
            arg = half * (half * half * B + A)
            act = half * jnp.tanh(arg) + half
            part = jnp.dot(wout_b[:, at:at + ROWS], act.astype(jnp.bfloat16), preferred_element_type=jnp.float32)
            total = part if total is None else total + part
        return total

    def prepare(group):
        for pair in range(per_dev // 2):
            rows = []
            for at in (2 * pair, 2 * pair + 1):
                scaled = win_f * mods[group, 0, at:at + 1, :].astype(jnp.float32)
                high = scaled.astype(jnp.bfloat16)
                low = (scaled - high.astype(jnp.float32)).astype(jnp.bfloat16)
                shift = jnp.broadcast_to(mods[group, 1, at:at + 1, :].astype(jnp.float32), win_f.shape)
                rows += [win_b, high, low, shift.astype(jnp.bfloat16)]
            weights[group * (per_dev // 2) + pair] = jnp.concatenate(rows, axis=0).T

    x0 = xv[...]
    rhs0 = rhs_of(x0, x0)
    for at, group in enumerate(order):
        if at > 0:
            for ref, send, recv in ((mods, mod_send, mod_recv), (steps, step_send, step_recv)):
                pltpu.make_async_remote_copy(
                    src_ref=ref.at[me], dst_ref=ref.at[group], send_sem=send.at[group], recv_sem=recv.at[group],
                    device_id={"time": group}, device_id_type=MESH).wait_recv()
        prepare(group)
        for pair in range(per_dev // 2):
            total = drift_of(group * (per_dev // 2) + pair, rhs0)
            for side in range(2):
                index = 2 * pair + side
                size = jnp.broadcast_to(steps[group][:, index:index + 1], (16, LANES))
                drifts[group * per_dev + index] = total[:, side * LANES:(side + 1) * LANES] * size

    n_steps = n_dev * per_dev
    latents = [x0]
    for index in range(n_steps - 1):
        latents.append(latents[-1] + drifts[index])

    out_copies = []
    for sweep in range(1, SWEEPS):
        last = sweep == SWEEPS - 1
        new = [x0]
        for index in range(sweep):
            new.append(latents[index + 1])
        for pair in range(n_steps // 2):
            wanted = [sweep <= index < n_steps - 1 for index in (2 * pair, 2 * pair + 1)]
            if any(wanted):
                values = [latents[2 * pair + side] if wanted[side] else None for side in range(2)]
                total = drift_of(pair, rhs_of(*values))
                column = 0
                for side in range(2):
                    if wanted[side]:
                        index = 2 * pair + side
                        size = jnp.broadcast_to(steps[index // per_dev][:, index % per_dev:index % per_dev + 1], (16, LANES))
                        new.append(new[-1] + total[:, column:column + LANES] * size)
                        column += LANES
        latents = new
    for index in range(n_steps):
        stage[index] = latents[index]
    place = (slice(None), sample, slice(None), pl.ds(first, LANES))
    for group in range(n_dev):
        copy = pltpu.make_async_remote_copy(
            src_ref=stage.at[pl.ds(group * per_dev, per_dev)], dst_ref=out_ref.at[place],
            send_sem=out_send.at[group], recv_sem=out_recv.at[me],
            device_id={"time": group}, device_id_type=MESH)

        @pl.when(me != group)
        def _():
            copy.start()

        @pl.when(me == group)
        def _():
            out_ref[place] = stage[group * per_dev:(group + 1) * per_dev]

    for copy in sends:
        copy.wait_send()
    for peer in peers:
        there = (slice(None), peer // 2, slice(None), pl.ds(pl.multiple_of(lax.rem(peer, 2) * LANES, LANES), LANES))
        done = pltpu.make_async_remote_copy(
            src_ref=stage.at[pl.ds(peer * per_dev, per_dev)], dst_ref=out_ref.at[there],
            send_sem=out_send.at[peer], recv_sem=out_recv.at[peer],
            device_id={"time": peer}, device_id_type=MESH)
        done.wait_send()
        done.wait_recv()


def solution(mesh):
    def local_run(x_init, w_in, w_out, mod_scale, mod_shift, step_size):
        samples, tokens, channels = x_init.shape
        per_dev, hidden = mod_scale.shape
        any_space = pl.BlockSpec(memory_space=pl.ANY)
        out = pl.pallas_call(
            kernel,
            out_shape=jax.ShapeDtypeStruct((per_dev, samples, channels, tokens), jnp.float32),
            in_specs=[any_space] * 6,
            out_specs=pl.BlockSpec(memory_space=pltpu.VMEM),
            scratch_shapes=[
                pltpu.VMEM((channels, LANES), jnp.float32),
                pltpu.VMEM((channels, hidden), jnp.bfloat16),
                pltpu.VMEM((channels, hidden), jnp.bfloat16),
                pltpu.VMEM((4, 2, per_dev, hidden), jnp.bfloat16),
                pltpu.VMEM((4, 1, per_dev), jnp.float32),
                pltpu.VMEM((2 * per_dev, hidden, LANES), jnp.bfloat16),
                pltpu.VMEM((4 * per_dev, channels, LANES), jnp.float32),
                pltpu.VMEM((4 * per_dev, channels, LANES), jnp.float32),
                pltpu.SemaphoreType.DMA((6,)),
                pltpu.SemaphoreType.DMA((4,)),
                pltpu.SemaphoreType.DMA((4,)),
                pltpu.SemaphoreType.DMA((4,)),
                pltpu.SemaphoreType.DMA((4,)),
                pltpu.SemaphoreType.DMA((4,)),
                pltpu.SemaphoreType.DMA((4,)),
            ],
            compiler_params=pltpu.CompilerParams(collective_id=0, has_side_effects=True),
        )(
            x_init.transpose(0, 2, 1), w_in, w_out.T, mod_scale, mod_shift,
            step_size.reshape(1, per_dev),
        )
        return out.transpose(0, 1, 3, 2)

    return jax.shard_map(
        local_run,
        mesh=mesh,
        in_specs=(P(("part", "data"), None, None), P(None, None), P(None, None), P("time", None), P("time", None), P("time")),
        out_specs=P("time", ("part", "data"), None, None),
        check_vma=False,
    )
```

time: 67.8 us -> 26.7 us (0.39)
  starting transfers between devices: 35.6 us -> 0 us
  Pallas kernels: 0 us -> 25 us
  matrix products: 17 us -> 0 us
  waiting for transfers between devices: 9.5 us -> 0 us
  other arithmetic: 4.98 us -> 0 us
  local copies, waits for them, and re-layouts: 0.04 us -> 1.57 us
    ppermute x8 -> x0, starting transfers between devices: 35.6 us -> none  [local_run(): inclusive = inclusive + lax.ppermute(inclusive, 'time', pairs)]
    pallas_call x0 -> x1, Pallas kernels: none -> 25 us  [local_run(): pl.pallas_call(kernel, out_shape=jax.ShapeDtypeStruct((per_dev, samples,...]
    dot_general x4 -> x0, matrix products: 17 us -> none  [drift_of(): jnp.einsum('kbnh,hc->kbnc', act.astype(jnp.bfloat16), w_out, preferred_el...]
    ppermute x8 -> x0, waiting for transfers between devices: 9.5 us -> none  [local_run(): inclusive = inclusive + lax.ppermute(inclusive, 'time', pairs)]
    another operation x4 -> x0, other arithmetic: 2.06 us -> none  [local_run(): running = jnp.cumsum(drift, axis=0)]
    unnamed x8 -> x1, local copies, waits for them, and re-layouts: 0.02 us -> 1.57 us
    convert_element_type x2 -> x0, other arithmetic: 1.47 us -> none  [the longest x1 0.77 us: drift_of(): latents.astype(jnp.bfloat16)]
    add x10 -> x0, other arithmetic: 1.45 us -> none  [the longest x5 0.72 us: local_run(): latents = x_init[None] + offset[None] + (running - drift)]
  transfers between devices with their start and end apart: 8 -> 0, of which waited for: 8 -> 0; matrix products, arithmetic and copies ran while one was open for 0% -> 0% of each run, Pallas kernels for 0% -> 0%
where the time goes in v1:
time: 26.7 us; the launch traced here: 26.6 us
  Pallas kernels  25 us (94%)
  local copies, waits for them, and re-layouts  1.57 us (6%)
    pallas_call x1, Pallas kernels, local_run(): pl.pallas_call(kernel, out_shape=jax.ShapeDtypeStruct((per_dev, samples,...  25 us
    unnamed x1, local copies, waits for them, and re-layouts  1.57 us

profile of v1, /device:TPU:0, one launch (start us, length us, event | category | flops | bytes accessed | tf_op | source)
XLA Modules:
  0.0 26.6 jit_solution(2874294187566019038)
XLA Ops:
  0.0 25.0 %shard_map.64 = f32[4,2,16,256]{3,2,1,0:T(8,128)} custom-call(f32[2,16,256]{2,1,0:T(8,128)} %bitcast.6, bf16[16,1152]{1,0:T(8,128)(2,1)} %win_hbm.1, bf16[16,1152]{1,0:T(8,128)(2,1)} %bitcast.5, bf16[4,1152]{1,0:T(4,128)(2,1)} %scale_hbm.1, bf16[4,1152]{1,0:T(4,128)(2,1)} %shift_hbm.1, f32[1,4]{1,0:T(1,128)} %bitcast.7), custom_call_target="tpu_custom_call" | custom-call | tf_op jit(solution)/shard_map/pallas_call | solution.py:175
  25.0 1.6 %copy.8 = f32[4,2,256,16]{2,3,1,0:T(8,128)} copy(f32[4,2,256,16]{2,3,1,0:T(8,128)} %bitcast.4) | data formatting | bytes 262144

commit v2 on v1

--- a/solution.py
+++ b/solution.py
@@ -11,6 +11,8 @@
 SWEEPS = 4
 LANES = 128
 ROWS = 128
+AHEAD = 5
+BEHIND = 1
 MESH = pl.DeviceIdType.MESH
 
 A = 2.0 * math.sqrt(2.0 / math.pi)
@@ -35,13 +37,13 @@
         pl.semaphore_signal(barrier, inc=1, device_id={"time": peer}, device_id_type=MESH)
 
     sample = me // 2
-    first = pl.multiple_of(lax.rem(me, 2) * LANES, LANES)
+    lane = pl.multiple_of(lax.rem(me, 2) * LANES, LANES)
     loads = [
         pltpu.make_async_copy(scale_hbm, mods.at[me, 0], local_sem.at[0]),
         pltpu.make_async_copy(shift_hbm, mods.at[me, 1], local_sem.at[1]),
         pltpu.make_async_copy(step_hbm, steps.at[me], local_sem.at[2]),
         pltpu.make_async_copy(win_hbm, win, local_sem.at[3]),
-        pltpu.make_async_copy(x_hbm.at[sample, :, pl.ds(first, LANES)], xv, local_sem.at[4]),
+        pltpu.make_async_copy(x_hbm.at[sample, :, pl.ds(lane, LANES)], xv, local_sem.at[4]),
         pltpu.make_async_copy(wout_hbm, wout, local_sem.at[5]),
     ]
     for load in loads:
@@ -77,15 +79,38 @@
             columns.append(jnp.concatenate(own + blank if at == 0 else blank + own, axis=0))
         return columns[0] if len(columns) == 1 else jnp.concatenate(columns, axis=1)
 
-    def drift_of(pair, rhs):
-        total = None
-        for at in range(0, hidden, ROWS):
-            half = jnp.dot(weights[pair, at:at + ROWS, :], rhs, preferred_element_type=jnp.float32)
+    chunks = list(range(0, hidden, ROWS))
+
+    def run(tasks):
+        todo = [(task, at) for task in tasks for at in chunks]
+        halves, acts, right, total = {}, {}, {}, {}
+
+        def first(step):
+            task, at = todo[step]
+            if at == 0:
+                right[id(task)] = task[1]()
+            halves[step] = jnp.dot(
+                weights[task[0], at:at + ROWS, :], right[id(task)], preferred_element_type=jnp.float32)
+
+        def second(step):
+            task, at = todo[step]
+            part = jnp.dot(wout_b[:, at:at + ROWS], acts.pop(step), preferred_element_type=jnp.float32)
+            total[id(task)] = part if at == 0 else total[id(task)] + part
+            if at == chunks[-1]:
+                task[2](total[id(task)])
+
+        for step in range(min(AHEAD, len(todo))):
+            first(step)
+        for step in range(len(todo)):
+            if step + AHEAD < len(todo):
+                first(step + AHEAD)
+            half = halves.pop(step)
             arg = half * (half * half * B + A)
-            act = half * jnp.tanh(arg) + half
-            part = jnp.dot(wout_b[:, at:at + ROWS], act.astype(jnp.bfloat16), preferred_element_type=jnp.float32)
-            total = part if total is None else total + part
-        return total
+            acts[step] = (half * jnp.tanh(arg) + half).astype(jnp.bfloat16)
+            if step >= BEHIND:
+                second(step - BEHIND)
+        for step in range(max(len(todo) - BEHIND, 0), len(todo)):
+            second(step)
 
     def prepare(group):
         for pair in range(per_dev // 2):
@@ -100,48 +125,64 @@
 
     x0 = xv[...]
     rhs0 = rhs_of(x0, x0)
-    for at, group in enumerate(order):
-        if at > 0:
-            for ref, send, recv in ((mods, mod_send, mod_recv), (steps, step_send, step_recv)):
-                pltpu.make_async_remote_copy(
-                    src_ref=ref.at[me], dst_ref=ref.at[group], send_sem=send.at[group], recv_sem=recv.at[group],
-                    device_id={"time": group}, device_id_type=MESH).wait_recv()
-        prepare(group)
-        for pair in range(per_dev // 2):
-            total = drift_of(group * (per_dev // 2) + pair, rhs0)
+
+    def wait_mods(group):
+        for ref, send, recv in ((mods, mod_send, mod_recv), (steps, step_send, step_recv)):
+            pltpu.make_async_remote_copy(
+                src_ref=ref.at[me], dst_ref=ref.at[group], send_sem=send.at[group], recv_sem=recv.at[group],
+                device_id={"time": group}, device_id_type=MESH).wait_recv()
+
+    def step_of(group, index):
+        return jnp.broadcast_to(steps[group][:, index:index + 1], (16, LANES))
+
+    def opening(group, pair):
+        def finish(total):
             for side in range(2):
                 index = 2 * pair + side
-                size = jnp.broadcast_to(steps[group][:, index:index + 1], (16, LANES))
-                drifts[group * per_dev + index] = total[:, side * LANES:(side + 1) * LANES] * size
+                drifts[group * per_dev + index] = total[:, side * LANES:(side + 1) * LANES] * step_of(group, index)
+
+        return (group * (per_dev // 2) + pair, lambda: rhs0, finish)
+
+    pairs = range(per_dev // 2)
+    prepare(order[0])
+    run([opening(order[0], pair) for pair in pairs])
+    wait_mods(order[1])
+    prepare(order[1])
+    run([opening(order[1], pair) for pair in pairs])
+    for group in order[2:]:
+        wait_mods(group)
+    for group in order[2:]:
+        prepare(group)
+    run([opening(group, pair) for group in order[2:] for pair in pairs])
 
     n_steps = n_dev * per_dev
     latents = [x0]
     for index in range(n_steps - 1):
         latents.append(latents[-1] + drifts[index])
-
-    out_copies = []
-    for sweep in range(1, SWEEPS):
-        last = sweep == SWEEPS - 1
-        new = [x0]
-        for index in range(sweep):
-            new.append(latents[index + 1])
-        for pair in range(n_steps // 2):
-            wanted = [sweep <= index < n_steps - 1 for index in (2 * pair, 2 * pair + 1)]
-            if any(wanted):
-                values = [latents[2 * pair + side] if wanted[side] else None for side in range(2)]
-                total = drift_of(pair, rhs_of(*values))
-                column = 0
-                for side in range(2):
-                    if wanted[side]:
-                        index = 2 * pair + side
-                        size = jnp.broadcast_to(steps[index // per_dev][:, index % per_dev:index % per_dev + 1], (16, LANES))
-                        new.append(new[-1] + total[:, column:column + LANES] * size)
-                        column += LANES
-        latents = new
-    for index in range(n_steps):
-        stage[index] = latents[index]
-    place = (slice(None), sample, slice(None), pl.ds(first, LANES))
-    for group in range(n_dev):
+    history = [latents]
+
+    def later(sweep, pair):
+        wanted = [side for side in range(2) if sweep <= 2 * pair + side < n_steps - 1]
+
+        def right():
+            return rhs_of(*[history[sweep - 1][2 * pair + side] if side in wanted else None for side in range(2)])
+
+        def finish(total):
+            new = history[sweep]
+            for at, side in enumerate(wanted):
+                index = 2 * pair + side
+                drift = total[:, at * LANES:(at + 1) * LANES] * step_of(index // per_dev, index % per_dev)
+                new.append(new[-1] + drift)
+                if sweep == SWEEPS - 1:
+                    stage[index + 1] = new[-1]
+                    if (index + 2) % per_dev == 0:
+                        give((index + 1) // per_dev)
+
+        return (pair, right, finish)
+
+    place = (slice(None), sample, slice(None), pl.ds(lane, LANES))
+
+    def give(group):
         copy = pltpu.make_async_remote_copy(
             src_ref=stage.at[pl.ds(group * per_dev, per_dev)], dst_ref=out_ref.at[place],
             send_sem=out_send.at[group], recv_sem=out_recv.at[me],
@@ -154,6 +195,32 @@
         @pl.when(me == group)
         def _():
             out_ref[place] = stage[group * per_dev:(group + 1) * per_dev]
+
+    tasks = []
+    for sweep in range(1, SWEEPS):
+        history.append(None)
+        for pair in range(n_steps // 2):
+            if 2 * pair + 1 >= sweep and 2 * pair < n_steps - 1:
+                tasks.append((sweep, pair))
+
+    def begin(sweep):
+        history[sweep] = list(history[sweep - 1][:sweep + 1])
+        if sweep == SWEEPS - 1:
+            for index in range(sweep + 1):
+                stage[index] = history[sweep][index]
+                if (index + 1) % per_dev == 0:
+                    give(index // per_dev)
+
+    def task_of(sweep, pair):
+        task = later(sweep, pair)
+        if 2 * pair <= sweep <= 2 * pair + 1:
+            def right():
+                begin(sweep)
+                return task[1]()
+            return (task[0], right, task[2])
+        return task
+
+    run([task_of(sweep, pair) for sweep, pair in tasks])
 
     for copy in sends:
         copy.wait_send()

time: 26.7 us -> 18.2 us (0.68)
  Pallas kernels: 25 us -> 16.5 us
    pallas_call x1, Pallas kernels: 25 us -> 16.5 us  [local_run(): pl.pallas_call(kernel, out_shape=jax.ShapeDtypeStruct((per_dev, samples,...]
where the time goes in v2:
time: 18.2 us; the launch traced here: 18 us
  Pallas kernels  16.5 us (91%)
  local copies, waits for them, and re-layouts  1.57 us (9%)
    pallas_call x1, Pallas kernels, local_run(): pl.pallas_call(kernel, out_shape=jax.ShapeDtypeStruct((per_dev, samples,...  16.5 us
    unnamed x1, local copies, waits for them, and re-layouts  1.57 us

profile of v2, /device:TPU:0, one launch (start us, length us, event | category | flops | bytes accessed | tf_op | source)
XLA Modules:
  0.0 18.0 jit_solution(8468874688111322754)
XLA Ops:
  0.0 16.5 %shard_map.64 = f32[4,2,16,256]{3,2,1,0:T(8,128)} custom-call(f32[2,16,256]{2,1,0:T(8,128)} %bitcast.6, bf16[16,1152]{1,0:T(8,128)(2,1)} %win_hbm.1, bf16[16,1152]{1,0:T(8,128)(2,1)} %bitcast.5, bf16[4,1152]{1,0:T(4,128)(2,1)} %scale_hbm.1, bf16[4,1152]{1,0:T(4,128)(2,1)} %shift_hbm.1, f32[1,4]{1,0:T(1,128)} %bitcast.7), custom_call_target="tpu_custom_call" | custom-call | tf_op jit(solution)/shard_map/pallas_call | solution.py:242
  16.5 1.6 %copy.8 = f32[4,2,256,16]{2,3,1,0:T(8,128)} copy(f32[4,2,256,16]{2,3,1,0:T(8,128)} %bitcast.4) | data formatting | bytes 262144

commit v3 on v0

v3 whole, which is shorter than its diff:
```python
import functools
import math

import jax
import jax.numpy as jnp
from jax import lax
from jax.experimental import pallas as pl
from jax.experimental.pallas import tpu as pltpu
from jax.sharding import PartitionSpec as P

SWEEPS = 4
ROWS = 128
LANES = 128
AHEAD = 5
BEHIND = 1
MESH = pl.DeviceIdType.MESH

A = 2.0 * math.sqrt(2.0 / math.pi)
B = 8.0 * math.sqrt(2.0 / math.pi) * 0.044715


def kernel(
    x_hbm, win_hbm, wout_hbm, scale_hbm, shift_hbm, step_hbm, out_ref,
    xs, win, wout, mods, scales, steps, weights, drifts, sums, sums_in, base_out, base_in, last_in,
    local_sem, pair_send, pair_recv, base_send, base_recv, last_send, last_recv, ready,
):
    me = lax.axis_index("time")
    chip, core = me // 2, lax.rem(me, 2)
    partner = 2 * chip + 1 - core
    far = 3 - me
    side = 2 * (1 - chip) + core
    sample = lax.rem(core + chip, 2)
    per_dev = mods.shape[2]
    hidden = win.shape[1]
    held = 2 * per_dev
    pairs = per_dev // 2

    barrier = pltpu.get_barrier_semaphore()
    pl.semaphore_signal(barrier, inc=1, device_id={"time": partner}, device_id_type=MESH)

    @pl.when(chip == 0)
    def _():
        for peer in (far, side):
            pl.semaphore_signal(barrier, inc=1, device_id={"time": peer}, device_id_type=MESH)

    loads = [
        pltpu.make_async_copy(source, target, local_sem.at[at])
        for at, (source, target) in enumerate((
            (scale_hbm, mods.at[core, 0]), (shift_hbm, mods.at[core, 1]), (step_hbm, steps.at[core]),
            (win_hbm, win), (x_hbm, xs), (wout_hbm, wout)))
    ]
    for load in loads:
        load.start()
    for load in loads[:3]:
        load.wait()
    pl.semaphore_wait(barrier, 1 + 2 * chip)

    def swap(at, ref, source):
        return pltpu.make_async_remote_copy(
            src_ref=ref.at[source], dst_ref=ref.at[source], send_sem=pair_send.at[at], recv_sem=pair_recv.at[at],
            device_id={"time": partner}, device_id_type=MESH)

    for at, ref in enumerate((mods, steps)):
        swap(at, ref, core).start()

    @pl.when(chip == 1)
    def _():
        for peer in (far, side):
            pl.semaphore_signal(ready.at[core], inc=1, device_id={"time": peer}, device_id_type=MESH)

    for load in loads[3:]:
        load.wait()

    def run(tasks):
        todo = [(task, at) for task in tasks for at in range(0, hidden, ROWS)]
        halves, acts, right, total = {}, {}, {}, {}

        def first(step):
            task, at = todo[step]
            if at == 0:
                right[id(task)] = task[1]()
            halves[step] = jnp.dot(
                weights[task[0], at:at + ROWS, :], right[id(task)], preferred_element_type=jnp.float32)

        def second(step):
            task, at = todo[step]
            part = jnp.dot(wout[:, at:at + ROWS], acts.pop(step), preferred_element_type=jnp.float32)
            total[id(task)] = part if at == 0 else total[id(task)] + part
            if at + ROWS == hidden:
                task[2](total[id(task)])

        for step in range(min(AHEAD, len(todo))):
            first(step)
        for step in range(len(todo)):
            if step + AHEAD < len(todo):
                first(step + AHEAD)
            half = halves.pop(step)
            arg = half * (half * half * B + A)
            acts[step] = (half * jnp.tanh(arg) + half).astype(jnp.bfloat16)
            if step >= BEHIND:
                second(step - BEHIND)
        for step in range(max(len(todo) - BEHIND, 0), len(todo)):
            second(step)

    def column(latent, index):
        half = (latent * 0.5).astype(jnp.bfloat16)
        row = lax.broadcasted_iota(jnp.int32, half.shape, 0)
        unit = jnp.where(row == index % per_dev, 0.5, 0.0).astype(jnp.bfloat16)
        blank = [jnp.zeros_like(half)] * 4
        own = [half, half, half, unit]
        return jnp.concatenate(own + blank if index % 2 == 0 else blank + own, axis=0)

    def beside(left, right):
        return jnp.concatenate([left, right], axis=1)

    def step_of(index, part=None):
        part = index // per_dev if part is None else part
        at = index % per_dev
        return jnp.broadcast_to(steps[part][:, at:at + 1], (xs.shape[1], LANES))

    def prepare(part):
        wide = win[...].astype(jnp.float32)
        scales[part] = mods[part, 0].astype(jnp.float32)
        shifts = jnp.concatenate(
            [mods[part, 1], jnp.zeros((wide.shape[0] - per_dev, hidden), jnp.bfloat16)], axis=0)
        for pair in range(pairs):
            rows = []
            for at in (2 * pair, 2 * pair + 1):
                scaled = wide * jnp.broadcast_to(scales[part, at:at + 1, :], wide.shape)
                high = scaled.astype(jnp.bfloat16)
                low = (scaled - high.astype(jnp.float32)).astype(jnp.bfloat16)
                rows += [win[...], high, low, shifts]
            weights[part * pairs + pair] = jnp.concatenate(rows, axis=0).T

    def start_of(half):
        return xs[sample, :, half * LANES:(half + 1) * LANES]

    other = 1 - core
    found = {}
    total_of = {}

    def drift_at(sweep, half, index):
        key = (sweep, half, index)
        return found[key] if key in found else drifts[half, index]

    def sum_before(sweep, half, index, settled):
        key = (sweep, half, index)
        if index == 0:
            return None
        if sweep > 0 and settled and index <= sweep:
            return sum_before(sweep - 1, half, index, settled)
        if key not in total_of:
            before = sum_before(sweep, half, index - 1, settled)
            drift = drift_at(sweep, half, index - 1)
            total_of[key] = drift if before is None else before + drift
        return total_of[key]

    def opening(done):
        def task(part, pair, half, fresh, last):
            def right():
                if fresh:
                    if part is other:
                        for at, ref in enumerate((mods, steps)):
                            swap(at, ref, other).wait_recv()
                    prepare(part)
                return beside(column(start_of(half), 2 * pair), column(start_of(half), 2 * pair + 1))

            def finish(total):
                for at in range(2):
                    index = 2 * pair + at
                    drifts[half, part * per_dev + index] = (
                        total[:, at * LANES:(at + 1) * LANES] * step_of(index, part))
                if last:
                    done(half)

            return (part * pairs + pair, right, finish)

        return [
            task(part, pair, half, half == 0 and pair == 0, part is other and pair == pairs - 1)
            for half in range(2) for part in (core, other) for pair in range(pairs)
        ]

    def add(base, part):
        return base if part is None else base + part

    def whole(sweep, index, latent, done=None):
        def finish(total):
            for half in range(2):
                found[sweep, half, index] = total[:, half * LANES:(half + 1) * LANES] * step_of(index)
            if done is not None:
                done()

        return (
            index // 2, lambda: beside(*[column(latent(sweep - 1, half, index), index) for half in range(2)]), finish)

    def paired(sweep, pair, half, latent, done=None):
        def finish(total):
            for at in range(2):
                found[sweep, half, 2 * pair + at] = total[:, at * LANES:(at + 1) * LANES] * step_of(2 * pair + at)
            if done is not None:
                done()

        return (
            pair, lambda: beside(*[column(latent(sweep - 1, half, 2 * pair + at), 2 * pair + at) for at in range(2)]),
            finish)

    def base_copy(sweep, half):
        place = (sweep, slice(None), pl.ds(half * LANES, LANES))
        return pltpu.make_async_remote_copy(
            src_ref=base_out.at[place], dst_ref=base_in.at[place], send_sem=base_send.at[2 * sweep + half],
            recv_sem=base_recv.at[2 * sweep + half], device_id={"time": far}, device_id_type=MESH)

    def last_copy(at, source):
        return pltpu.make_async_remote_copy(
            src_ref=base_out.at[SWEEPS - 1], dst_ref=last_in.at[source], send_sem=last_send.at[at],
            recv_sem=last_recv.at[source], device_id={"time": (far, side)[at]}, device_id_type=MESH)

    def sums_copy():
        return pltpu.make_async_remote_copy(
            src_ref=sums.at[pl.ds((1 - core) * per_dev, per_dev)], dst_ref=sums_in, send_sem=pair_send.at[2],
            recv_sem=pair_recv.at[2], device_id={"time": partner}, device_id_type=MESH)

    def share(settled):
        for index in range(held):
            for half in range(2):
                value = sum_before(SWEEPS - 1, half, index, settled)
                sums[index, :, half * LANES:(half + 1) * LANES] = (
                    jnp.zeros((xs.shape[1], LANES), jnp.float32) if value is None else value)
        sums_copy().start()

    def close(bases):
        out_ref[:, sample] = bases[sample] + sums[pl.ds(core * per_dev, per_dev)]
        sums_copy().wait_recv()
        out_ref[:, 1 - sample] = bases[1 - sample] + sums_in[...]

    @pl.when(chip == 0)
    def _():
        found.clear(), total_of.clear()

        def latent(sweep, half, index):
            return add(start_of(half), sum_before(sweep, half, index, True))

        def put(sweep, half):
            base_out[sweep, :, half * LANES:(half + 1) * LANES] = latent(sweep, half, held)

        def send(sweep, half):
            put(sweep, half)
            if sweep == half == 0:
                pl.semaphore_wait(ready.at[1 - core], 1)
            base_copy(sweep, half).start()

        def send_last():
            put(SWEEPS - 1, 0), put(SWEEPS - 1, 1)
            pl.semaphore_wait(ready.at[core], 1)
            for at in range(2):
                last_copy(at, sample).start()

        tasks = opening(lambda half: send(0, half))
        for sweep in range(1, SWEEPS - 1):
            odd = sweep % 2 == 1
            for half in range(2):
                many = list(range((sweep + 1) // 2, held // 2))
                for pair in many:
                    close_now = pair == many[-1] and not (odd and half == 0)
                    tasks.append(paired(
                        sweep, pair, half, latent, functools.partial(send, sweep, half) if close_now else None))
                if odd and half == 0:
                    tasks.append(whole(sweep, sweep, latent, functools.partial(send, sweep, half)))
        tasks += [
            whole(SWEEPS - 1, index, latent, send_last if index == held - 1 else None)
            for index in range(SWEEPS - 1, held)]
        run(tasks)
        share(True)
        close(xs)
        for sweep in range(SWEEPS - 1):
            for half in range(2):
                base_copy(sweep, half).wait_send()
        for at in range(2):
            last_copy(at, sample).wait_send()

    @pl.when(chip == 1)
    def _():
        found.clear(), total_of.clear()
        arrived = set()

        def latent(sweep, half, index):
            if sweep < 0:
                return start_of(half)
            if (sweep, half) not in arrived:
                arrived.add((sweep, half))
                base_copy(sweep, half).wait_recv()
            base = base_in[sweep, :, half * LANES:(half + 1) * LANES]
            return add(base, sum_before(sweep, half, index, False))

        for at, ref in enumerate((mods, steps)):
            swap(at, ref, other).wait_recv()
        prepare(0)
        prepare(1)
        tasks = []
        for sweep in range(SWEEPS):
            live = per_dev + sweep
            tasks += [paired(sweep, pair, half, latent) for half in range(2) for pair in range(live // 2)]
            if live % 2 == 1:
                tasks.append(whole(sweep, live - 1, latent))
        run(tasks)
        share(False)
        for source in range(2):
            last_copy(0, source).wait_recv()
        close(last_in)

    for at, ref in enumerate((mods, steps)):
        swap(at, ref, core).wait_send()
    sums_copy().wait_send()


def solution(mesh):
    def local_run(x_init, w_in, w_out, mod_scale, mod_shift, step_size):
        samples, tokens, channels = x_init.shape
        per_dev, hidden = mod_scale.shape
        held = 2 * per_dev
        operands = (
            x_init.transpose(0, 2, 1), w_in, w_out.T, mod_scale, mod_shift, step_size.reshape(1, per_dev))
        latent = (channels, tokens)
        out = pl.pallas_call(
            kernel,
            out_shape=pltpu.VMEM((per_dev, samples) + latent, jnp.float32),
            in_specs=[pl.BlockSpec(memory_space=pl.ANY)] * len(operands),
            out_specs=pl.BlockSpec(memory_space=pltpu.VMEM),
            scratch_shapes=[
                pltpu.VMEM((samples,) + latent, jnp.float32),
                pltpu.VMEM((channels, hidden), jnp.bfloat16),
                pltpu.VMEM((channels, hidden), jnp.bfloat16),
                pltpu.VMEM((2, 2, per_dev, hidden), jnp.bfloat16),
                pltpu.VMEM((2, per_dev, hidden), jnp.float32),
                pltpu.VMEM((2, 1, per_dev), jnp.float32),
                pltpu.VMEM((per_dev, hidden, LANES), jnp.bfloat16),
                pltpu.VMEM((2, held, channels, LANES), jnp.float32),
                pltpu.VMEM((held,) + latent, jnp.float32),
                pltpu.VMEM((per_dev,) + latent, jnp.float32),
                pltpu.VMEM((SWEEPS,) + latent, jnp.float32),
                pltpu.VMEM((SWEEPS - 1,) + latent, jnp.float32),
                pltpu.VMEM((samples,) + latent, jnp.float32),
                pltpu.SemaphoreType.DMA((6,)),
                pltpu.SemaphoreType.DMA((3,)),
                pltpu.SemaphoreType.DMA((3,)),
                pltpu.SemaphoreType.DMA((2 * SWEEPS - 2,)),
                pltpu.SemaphoreType.DMA((2 * SWEEPS - 2,)),
                pltpu.SemaphoreType.DMA((2,)),
                pltpu.SemaphoreType.DMA((2,)),
                pltpu.SemaphoreType.REGULAR((2,)),
            ],
            compiler_params=pltpu.CompilerParams(
                collective_id=0, has_side_effects=True, vmem_limit_bytes=32 << 20),
        )(*[pltpu.with_memory_space_constraint(operand, pltpu.HBM) for operand in operands])
        return out.transpose(0, 1, 3, 2)

    return jax.shard_map(
        local_run,
        mesh=mesh,
        in_specs=(P(("part", "data"), None, None), P(None, None), P(None, None), P("time", None), P("time", None), P("time")),
        out_specs=P("time", ("part", "data"), None, None),
        check_vma=False,
    )
```

time: 67.8 us -> 14.3 us (0.21)
  the two profiles are of different devices: /device:TPU:0 before, /device:TPU:7 now
where the time goes in v3:
time: 14.3 us; the launch traced here: 14.2 us
  Pallas kernels  13.5 us (94%)
  local copies, waits for them, and re-layouts  0.66 us (5%)
    pallas_call x1, Pallas kernels, local_run(): pl.pallas_call(kernel, out_shape=pltpu.VMEM((per_dev, samples) + latent,...  13.5 us
    unnamed x1, local copies, waits for them, and re-layouts  0.66 us

profile of v3, /device:TPU:7, one launch (start us, length us, event | category | flops | bytes accessed | tf_op | source)
XLA Modules:
  0.0 14.2 jit_solution(10513248052259110374)
XLA Ops:
  0.0 13.5 %shard_map.64 = f32[4,2,16,256]{3,2,1,0:T(8,128)S(1)} custom-call(f32[2,16,256]{2,1,0:T(8,128)} %bitcast.6, bf16[16,1152]{1,0:T(8,128)(2,1)} %win_hbm.1, bf16[16,1152]{1,0:T(8,128)(2,1)} %bitcast.5, bf16[4,1152]{1,0:T(4,128)(2,1)} %scale_hbm.1, bf16[4,1152]{1,0:T(4,128)(2,1)} %shift_hbm.1, f32[1,4]{1,0:T(1,128)} %bitcast.7), custom_call_target="tpu_custom_call" | custom-call | tf_op jit(solution)/shard_map/pallas_call | solution.py:324
  13.5 0.7 %copy.8 = f32[4,2,256,16]{2,3,1,0:T(8,128)} copy(f32[4,2,256,16]{2,3,1,0:T(8,128)S(1)} %bitcast.4) | data formatting | bytes 262144

commit v4 on v3

--- a/solution.py
+++ b/solution.py
@@ -9,9 +9,9 @@
 from jax.sharding import PartitionSpec as P
 
 SWEEPS = 4
-ROWS = 128
+ROWS = 192
 LANES = 128
-AHEAD = 5
+AHEAD = 3
 BEHIND = 1
 MESH = pl.DeviceIdType.MESH
 
@@ -21,7 +21,7 @@
 
 def kernel(
     x_hbm, win_hbm, wout_hbm, scale_hbm, shift_hbm, step_hbm, out_ref,
-    xs, win, wout, mods, scales, steps, weights, drifts, sums, sums_in, base_out, base_in, last_in,
+    xs, win, wout, mods, scales, steps, weights, drifts, sums, sums_in, base_out, base_in, last_in, hand_out, hand_in,
     local_sem, pair_send, pair_recv, base_send, base_recv, last_send, last_recv, ready,
 ):
     me = lax.axis_index("time")
@@ -210,28 +210,28 @@
             src_ref=base_out.at[place], dst_ref=base_in.at[place], send_sem=base_send.at[2 * sweep + half],
             recv_sem=base_recv.at[2 * sweep + half], device_id={"time": far}, device_id_type=MESH)
 
-    def last_copy(at, source):
+    def last_copy(at, source, half):
+        lanes = pl.ds(half * LANES, LANES)
         return pltpu.make_async_remote_copy(
-            src_ref=base_out.at[SWEEPS - 1], dst_ref=last_in.at[source], send_sem=last_send.at[at],
-            recv_sem=last_recv.at[source], device_id={"time": (far, side)[at]}, device_id_type=MESH)
-
-    def sums_copy():
+            src_ref=base_out.at[SWEEPS - 1, :, lanes], dst_ref=last_in.at[source, :, lanes],
+            send_sem=last_send.at[2 * at + half], recv_sem=last_recv.at[2 * source + half],
+            device_id={"time": (far, side)[at]}, device_id_type=MESH)
+
+    def sums_copy(start, count):
         return pltpu.make_async_remote_copy(
-            src_ref=sums.at[pl.ds((1 - core) * per_dev, per_dev)], dst_ref=sums_in, send_sem=pair_send.at[2],
+            src_ref=sums.at[pl.ds(start, count)], dst_ref=sums_in.at[pl.ds(0, count)], send_sem=pair_send.at[2],
             recv_sem=pair_recv.at[2], device_id={"time": partner}, device_id_type=MESH)
 
-    def share(settled):
-        for index in range(held):
-            for half in range(2):
-                value = sum_before(SWEEPS - 1, half, index, settled)
-                sums[index, :, half * LANES:(half + 1) * LANES] = (
-                    jnp.zeros((xs.shape[1], LANES), jnp.float32) if value is None else value)
-        sums_copy().start()
-
-    def close(bases):
-        out_ref[:, sample] = bases[sample] + sums[pl.ds(core * per_dev, per_dev)]
-        sums_copy().wait_recv()
-        out_ref[:, 1 - sample] = bases[1 - sample] + sums_in[...]
+    def hand_copy():
+        return pltpu.make_async_remote_copy(
+            src_ref=hand_out, dst_ref=hand_in, send_sem=pair_send.at[3],
+            recv_sem=pair_recv.at[3], device_id={"time": partner}, device_id_type=MESH)
+
+    def whole_sum(index, settled):
+        values = [sum_before(SWEEPS - 1, half, index, settled) for half in range(2)]
+        if values[0] is None:
+            return jnp.zeros(xs.shape[1:], jnp.float32)
+        return beside(*values)
 
     @pl.when(chip == 0)
     def _():
@@ -249,11 +249,12 @@
                 pl.semaphore_wait(ready.at[1 - core], 1)
             base_copy(sweep, half).start()
 
-        def send_last():
-            put(SWEEPS - 1, 0), put(SWEEPS - 1, 1)
-            pl.semaphore_wait(ready.at[core], 1)
+        def send_last(half):
+            put(SWEEPS - 1, half)
+            if half == 0:
+                pl.semaphore_wait(ready.at[core], 1)
             for at in range(2):
-                last_copy(at, sample).start()
+                last_copy(at, sample, half).start()
 
         tasks = opening(lambda half: send(0, half))
         for sweep in range(1, SWEEPS - 1):
@@ -266,22 +267,33 @@
                         sweep, pair, half, latent, functools.partial(send, sweep, half) if close_now else None))
                 if odd and half == 0:
                     tasks.append(whole(sweep, sweep, latent, functools.partial(send, sweep, half)))
-        tasks += [
-            whole(SWEEPS - 1, index, latent, send_last if index == held - 1 else None)
-            for index in range(SWEEPS - 1, held)]
+        tasks.append(whole(SWEEPS - 1, SWEEPS - 1, latent))
+        for half in range(2):
+            for pair in range(SWEEPS // 2, held // 2):
+                tasks.append(paired(
+                    SWEEPS - 1, pair, half, latent,
+                    functools.partial(send_last, half) if pair == held // 2 - 1 else None))
         run(tasks)
-        share(True)
-        close(xs)
+        for index in range(held):
+            sums[index] = whole_sum(index, True)
+        sums_copy(other * per_dev, per_dev).start()
+        out_ref[:, sample] = xs[sample] + sums[pl.ds(core * per_dev, per_dev)]
+        sums_copy(0, per_dev).wait_recv()
+        out_ref[:, 1 - sample] = xs[1 - sample] + sums_in[...]
         for sweep in range(SWEEPS - 1):
             for half in range(2):
                 base_copy(sweep, half).wait_send()
         for at in range(2):
-            last_copy(at, sample).wait_send()
-
-    @pl.when(chip == 1)
-    def _():
+            for half in range(2):
+                last_copy(at, sample, half).wait_send()
+        sums_copy(0, per_dev).wait_send()
+
+    def second_chip(which):
         found.clear(), total_of.clear()
         arrived = set()
+        mine, theirs = (1 + which) % 2, which % 2
+        last = SWEEPS - 1
+        lent = {}
 
         def latent(sweep, half, index):
             if sweep < 0:
@@ -292,6 +304,27 @@
             base = base_in[sweep, :, half * LANES:(half + 1) * LANES]
             return add(base, sum_before(sweep, half, index, False))
 
+        def hand():
+            for half in range(2):
+                hand_out[:, half * LANES:(half + 1) * LANES] = latent(last - 1, half, held - 2)
+            hand_copy().start()
+
+        def early():
+            for index in range(per_dev):
+                sums[index] = whole_sum(index, False)
+            sums_copy(0, per_dev).start()
+
+        def extra():
+            def right():
+                hand_copy().wait_recv()
+                return beside(*[
+                    column(hand_in[:, half * LANES:(half + 1) * LANES], held - 2) for half in range(2)])
+
+            def finish(total):
+                lent[0] = total * beside(step_of(held - 2), step_of(held - 2))
+
+            return (held // 2 - 1, right, finish)
+
         for at, ref in enumerate((mods, steps)):
             swap(at, ref, other).wait_recv()
         prepare(0)
@@ -299,18 +332,46 @@
         tasks = []
         for sweep in range(SWEEPS):
             live = per_dev + sweep
-            tasks += [paired(sweep, pair, half, latent) for half in range(2) for pair in range(live // 2)]
-            if live % 2 == 1:
+            for half in range(2):
+                for pair in range(live // 2):
+                    done = None
+                    if sweep == last and half == 1 and pair == 0 and which == 0:
+                        done = hand
+                    if sweep == last and half == 1 and pair == per_dev // 2 - 1 and which == 1:
+                        done = early
+                    tasks.append(paired(sweep, pair, half, latent, done))
+            if live % 2 == 1 and not (sweep == last and which == 0):
                 tasks.append(whole(sweep, live - 1, latent))
+        if which == 1:
+            tasks.append(extra())
         run(tasks)
-        share(False)
+        if which == 0:
+            for index in range(per_dev, held - 1):
+                sums[index] = whole_sum(index, False)
+            sums_copy(per_dev, per_dev - 1).start()
         for source in range(2):
-            last_copy(0, source).wait_recv()
-        close(last_in)
+            for half in range(2):
+                last_copy(0, source, half).wait_recv()
+        for index in range(per_dev):
+            out_ref[index, mine] = last_in[mine] + whole_sum(which * per_dev + index, False)
+        if which == 0:
+            sums_copy(0, per_dev).wait_recv()
+            out_ref[:, theirs] = last_in[theirs] + sums_in[...]
+            hand_copy().wait_send()
+            sums_copy(0, per_dev - 1).wait_send()
+        else:
+            sums_copy(0, per_dev - 1).wait_recv()
+            out_ref[:per_dev - 1, theirs] = last_in[theirs] + sums_in[:per_dev - 1]
+            out_ref[per_dev - 1, theirs] = last_in[theirs] + (sums_in[per_dev - 2] + lent[0])
+            sums_copy(0, per_dev).wait_send()
+
+    for which in range(2):
+        @pl.when(me == 2 + which)
+        def _():
+            second_chip(which)
 
     for at, ref in enumerate((mods, steps)):
         swap(at, ref, core).wait_send()
-    sums_copy().wait_send()
 
 
 def solution(mesh):
@@ -340,13 +401,15 @@
                 pltpu.VMEM((SWEEPS,) + latent, jnp.float32),
                 pltpu.VMEM((SWEEPS - 1,) + latent, jnp.float32),
                 pltpu.VMEM((samples,) + latent, jnp.float32),
+                pltpu.VMEM(latent, jnp.float32),
+                pltpu.VMEM(latent, jnp.float32),
                 pltpu.SemaphoreType.DMA((6,)),
-                pltpu.SemaphoreType.DMA((3,)),
-                pltpu.SemaphoreType.DMA((3,)),
+                pltpu.SemaphoreType.DMA((4,)),
+                pltpu.SemaphoreType.DMA((4,)),
                 pltpu.SemaphoreType.DMA((2 * SWEEPS - 2,)),
                 pltpu.SemaphoreType.DMA((2 * SWEEPS - 2,)),
-                pltpu.SemaphoreType.DMA((2,)),
-                pltpu.SemaphoreType.DMA((2,)),
+                pltpu.SemaphoreType.DMA((4,)),
+                pltpu.SemaphoreType.DMA((4,)),
                 pltpu.SemaphoreType.REGULAR((2,)),
             ],
             compiler_params=pltpu.CompilerParams(

time: 14.3 us -> 13.8 us (0.965)
  the two profiles are of different devices: /device:TPU:7 before, /device:TPU:0 now
where the time goes in v4:
time: 13.8 us; the launch traced here: 13.6 us
  Pallas kernels  12.9 us (93%)
  local copies, waits for them, and re-layouts  0.66 us (5%)
    pallas_call x1, Pallas kernels, local_run(): pl.pallas_call(kernel, out_shape=pltpu.VMEM((per_dev, samples) + latent,...  12.9 us
    unnamed x1, local copies, waits for them, and re-layouts  0.66 us

profile of v4, /device:TPU:0, one launch (start us, length us, event | category | flops | bytes accessed | tf_op | source)
XLA Modules:
  0.0 13.6 jit_solution(2817637088132127178)
XLA Ops:
  0.0 12.9 %shard_map.64 = f32[4,2,16,256]{3,2,1,0:T(8,128)S(1)} custom-call(f32[2,16,256]{2,1,0:T(8,128)} %bitcast.6, bf16[16,1152]{1,0:T(8,128)(2,1)} %win_hbm.1, bf16[16,1152]{1,0:T(8,128)(2,1)} %bitcast.5, bf16[4,1152]{1,0:T(4,128)(2,1)} %scale_hbm.1, bf16[4,1152]{1,0:T(4,128)(2,1)} %shift_hbm.1, f32[1,4]{1,0:T(1,128)} %bitcast.7), custom_call_target="tpu_custom_call" | custom-call | tf_op jit(solution)/shard_map/pallas_call | solution.py:385
  12.9 0.7 %copy.8 = f32[4,2,256,16]{2,3,1,0:T(8,128)} copy(f32[4,2,256,16]{2,3,1,0:T(8,128)S(1)} %bitcast.4) | data formatting | bytes 262144

commit v5 on v4

--- a/solution.py
+++ b/solution.py
@@ -9,7 +9,7 @@
 from jax.sharding import PartitionSpec as P
 
 SWEEPS = 4
-ROWS = 192
+ROWS = 256
 LANES = 128
 AHEAD = 3
 BEHIND = 1
@@ -72,21 +72,21 @@
         load.wait()
 
     def run(tasks):
-        todo = [(task, at) for task in tasks for at in range(0, hidden, ROWS)]
+        todo = [(task, slice(at, min(at + ROWS, hidden))) for task in tasks for at in range(0, hidden, ROWS)]
         halves, acts, right, total = {}, {}, {}, {}
 
         def first(step):
             task, at = todo[step]
-            if at == 0:
+            if at.start == 0:
                 right[id(task)] = task[1]()
             halves[step] = jnp.dot(
-                weights[task[0], at:at + ROWS, :], right[id(task)], preferred_element_type=jnp.float32)
+                weights[task[0], at, :], right[id(task)], preferred_element_type=jnp.float32)
 
         def second(step):
             task, at = todo[step]
-            part = jnp.dot(wout[:, at:at + ROWS], acts.pop(step), preferred_element_type=jnp.float32)
-            total[id(task)] = part if at == 0 else total[id(task)] + part
-            if at + ROWS == hidden:
+            part = jnp.dot(wout[:, at], acts.pop(step), preferred_element_type=jnp.float32)
+            total[id(task)] = part if at.start == 0 else total[id(task)] + part
+            if at.stop == hidden:
                 task[2](total[id(task)])
 
         for step in range(min(AHEAD, len(todo))):
@@ -177,7 +177,7 @@
 
         return [
             task(part, pair, half, half == 0 and pair == 0, part is other and pair == pairs - 1)
-            for half in range(2) for part in (core, other) for pair in range(pairs)
+            for part in (core, other) for half in range(2) for pair in range(pairs)
         ]
 
     def add(base, part):

time: 13.8 us -> 13.6 us (0.986)
  the two profiles are of different devices: /device:TPU:0 before, /device:TPU:7 now
where the time goes in v5:
time: 13.6 us; the launch traced here: 13.4 us
  Pallas kernels  12.7 us (93%)
  local copies, waits for them, and re-layouts  0.66 us (5%)
    pallas_call x1, Pallas kernels, local_run(): pl.pallas_call(kernel, out_shape=pltpu.VMEM((per_dev, samples) + latent,...  12.7 us
    unnamed x1, local copies, waits for them, and re-layouts  0.66 us

profile of v5, /device:TPU:7, one launch (start us, length us, event | category | flops | bytes accessed | tf_op | source)
XLA Modules:
  0.0 13.4 jit_solution(9492791424520098687)
XLA Ops:
  0.0 12.7 %shard_map.64 = f32[4,2,16,256]{3,2,1,0:T(8,128)S(1)} custom-call(f32[2,16,256]{2,1,0:T(8,128)} %bitcast.6, bf16[16,1152]{1,0:T(8,128)(2,1)} %win_hbm.1, bf16[16,1152]{1,0:T(8,128)(2,1)} %bitcast.5, bf16[4,1152]{1,0:T(4,128)(2,1)} %scale_hbm.1, bf16[4,1152]{1,0:T(4,128)(2,1)} %shift_hbm.1, f32[1,4]{1,0:T(1,128)} %bitcast.7), custom_call_target="tpu_custom_call" | custom-call | tf_op jit(solution)/shard_map/pallas_call | solution.py:385
  12.7 0.7 %copy.8 = f32[4,2,256,16]{2,3,1,0:T(8,128)} copy(f32[4,2,256,16]{2,3,1,0:T(8,128)S(1)} %bitcast.4) | data formatting | bytes 262144
